TPU v7x, 32 devices: a whole 2x2x4 slice. The times are simulated.
32 devices in a mesh: heads: 4 (over y, core), blk: 8 (over z, x).
Axes of the slice: x: 2, y: 2, z: 4, core: 2. Of those that a mesh axis runs over, the one named last changes fastest.
Arguments:
- tokens: bfloat16 [4096, 4096], P(('blk', 'heads')), may hold values from -6 to 6
- w_query: bfloat16 [4096, 2048], P('blk', 'heads'), may hold values from -0.75 to 0.75
- key_value_weight: bfloat16 [4096, 2, 512], P('blk', None, 'heads'), may hold values from -0.75 to 0.75
- w_out: bfloat16 [2048, 4096], P(('heads', 'blk')), may hold values from -0.5 to 0.5
- doc_lengths: int32 [16], replicated, may hold values from 1 to 1024, 4096 in all
Outputs:
- attended: bfloat16 [4096, 4096], P(('blk', 'heads'))
Inputs may be any that keep to these rules, and one draw needn't show every extreme that they name: `doc_lengths`: the 16 lengths sum to 4096; the longest document has exactly 1024 tokens.
All inputs are finite; a program needn't handle non-finite values.
Results may differ from a plain program's by a relative error of at most 0.012.
Values may be sent and summed in bfloat16 or wider, within the bound.
A program may use at most 128 MiB of HBM per device.

v0:
```python
import jax
import jax.numpy as jnp
from jax import lax
from jax.sharding import PartitionSpec as P

HEAD_SIZE = 128
norm_epsilon = 1e-05
rope_base = 500000.0
masked_score = -1e30


def shifted(value, axis, steps):
    count = lax.axis_size(axis)
    first, last = (max(0, -steps), min(count, count - steps))
    return lax.ppermute(value, axis, [(source, source + steps) for source in range(first, last)])


def locate_documents(positions, doc_lengths):
    ends = jnp.cumsum(doc_lengths)
    after = positions[:, None] >= ends[None, :]
    ident = jnp.sum(after.astype(jnp.int32), axis=1)
    starts = jnp.sum(jnp.where(after, doc_lengths[None, :], 0), axis=1)
    return (ident, starts)


def apply_rotation(values, relative_offset):
    half = values.shape[-1] // 2
    freqs = jnp.power(rope_base, -2.0 * jnp.arange(half, dtype=jnp.float32) / values.shape[-1])
    angle = relative_offset.astype(jnp.float32)[:, None] * freqs[None, :]
    cosine = jnp.cos(angle)[:, None, :]
    sine = jnp.sin(angle)[:, None, :]
    first = values[..., :half]
    second = values[..., half:]
    return jnp.concatenate(
        [first * cosine - second * sine, second * cosine + first * sine], axis=-1
    )


def on_device(tokens, w_query, key_value_weight, w_out, doc_lengths):
    blk_index = lax.axis_index("blk")
    reach = lax.axis_size("blk") // 4
    values = tokens.astype(jnp.float32)
    normalized_input = (
        values * lax.rsqrt(jnp.mean(values * values, axis=1, keepdims=True) + norm_epsilon)
    ).astype(jnp.bfloat16)
    block_input = lax.all_gather(normalized_input, "heads", axis=0, tiled=True)
    block_rows = block_input.shape[0]
    query_cols = w_query.shape[1]
    kv_cols = key_value_weight.shape[2]
    pieces = (
        lax.all_gather(w_query, "blk", axis=0, tiled=True),
        lax.all_gather(key_value_weight, "blk", axis=0, tiled=True),
    )
    count = pieces[0].shape[0]
    query_part = jnp.dot(block_input, pieces[0], preferred_element_type=jnp.float32)
    keyval_part = jnp.dot(
        block_input, pieces[1].reshape(count, 2 * kv_cols), preferred_element_type=jnp.float32
    )
    positions = blk_index * block_rows + jnp.arange(block_rows, dtype=jnp.int32)
    ident, starts = locate_documents(positions, doc_lengths)
    relative_offset = positions - starts
    query_heads = query_cols // HEAD_SIZE
    kv_heads = kv_cols // HEAD_SIZE
    head_group = query_heads // kv_heads
    query_rows = apply_rotation(
        query_part.reshape(block_rows, query_heads, HEAD_SIZE), relative_offset
    ).astype(jnp.bfloat16)
    query_rows = query_rows.reshape(block_rows, kv_heads, head_group, HEAD_SIZE)
    rotated_keys = apply_rotation(
        keyval_part[:, :kv_cols].reshape(block_rows, kv_heads, HEAD_SIZE), relative_offset
    ).astype(jnp.bfloat16)
    value_rows = (
        keyval_part[:, kv_cols:].reshape(block_rows, kv_heads, HEAD_SIZE).astype(jnp.bfloat16)
    )
    kv_block = jnp.stack([rotated_keys, value_rows], axis=1)
    scale = HEAD_SIZE ** (-0.5)

    def attend_tile(state, kv_now, distance):
        key_pos = (blk_index - distance) * block_rows + jnp.arange(block_rows, dtype=jnp.int32)
        key_doc, unused_k = locate_documents(key_pos, doc_lengths)
        keep = (
            (key_pos[None, :] >= 0)
            & (key_pos[None, :] <= positions[:, None])
            & (key_doc[None, :] == ident[:, None])
        )
        highest, totals, accum = state
        scores = (
            jnp.einsum(
                "qhgd,khd->hgqk", query_rows, kv_now[:, 0], preferred_element_type=jnp.float32
            )
            * scale
        )
        scores = jnp.where(keep, scores, masked_score)
        new_high = jnp.maximum(highest, jnp.max(scores, axis=-1))
        fading = jnp.exp(highest - new_high)
        probs = jnp.where(keep, jnp.exp(scores - new_high[..., None]), 0.0)
        totals = totals * fading + jnp.sum(probs, axis=-1)
        update = jnp.einsum(
            "hgqk,khd->hgqd",
            probs.astype(jnp.bfloat16),
            kv_now[:, 1],
            preferred_element_type=jnp.float32,
        )
        accum = accum * fading[..., None] + update
        return (new_high, totals, accum)

    initial = (
        jnp.full((kv_heads, head_group, block_rows), masked_score, jnp.float32),
        jnp.zeros((kv_heads, head_group, block_rows), jnp.float32),
        jnp.zeros((kv_heads, head_group, block_rows, HEAD_SIZE), jnp.float32),
    )
    state = attend_tile(initial, kv_block, 0)

    def advance(distance, carry):
        kv_now, inner = carry
        kv_now = shifted(kv_now, "blk", 1)
        return (kv_now, attend_tile(inner, kv_now, distance))

    unused_kv, state = lax.fori_loop(1, reach + 1, advance, (kv_block, state))
    highest, totals, accum = state
    mixed = accum / totals[..., None]
    mixed = mixed.transpose(2, 0, 1, 3).reshape(block_rows, query_cols).astype(jnp.bfloat16)
    head_rows = lax.all_gather(w_out, "blk", axis=0, tiled=True)
    return lax.psum_scatter(
        jnp.dot(mixed, head_rows, preferred_element_type=jnp.float32).astype(jnp.bfloat16),
        "heads",
        scatter_dimension=0,
        tiled=True,
    )


def solution(mesh):
    return jax.shard_map(
        on_device,
        mesh=mesh,
        in_specs=(
            P(("blk", "heads"), None),
            P("blk", "heads"),
            P("blk", None, "heads"),
            P(("heads", "blk"), None),
            P(),
        ),
        out_specs=P(("blk", "heads"), None),
        check_vma=False,
    )
```

profile of v0, /device:TPU:0, one launch (start us, length us, event | category | flops | bytes accessed | tf_op | source)
XLA Modules:
  0.0 311.8 jit_solution(1493680241664175790)
XLA Ops:
  6.5 0.7 all-gather.7.cloned.1.call-update
  7.3 0.0 all-gather.5.cloned.1.call-start
  7.3 1.5 fusion.24
  8.8 2.5 fusion.25
  11.3 0.0 all-gather.9.cloned.1.call-start
  11.4 0.7 all-gather.9.cloned.1.call-update
  12.1 0.5 all-gather.11.cloned.1.call-update
  12.6 0.0 reduce-scatter.2.cloned.1.call-start
  12.7 0.2 broadcast_in_dim.114
  12.9 0.1 fusion.56
  13.0 1.0 multiply_cosine_fusion
  14.0 0.4 compare_and_fusion.1
  14.4 46.9 %all-gather.7.cloned.1.call-done = bf16[4096,2,128]{2,1,0:T(2,128)(2,1)} async-done(((bf16[512,2,128]{2,1,0:T(2,128)(2,1)}), bf16[4096,2,128]{2,1,0:T(2,128)(2,1)}) %all-gather.7.cloned.1.call-update) | async-done | bytes 2097168 | tf_op jit(solution)/shard_map/all_gather | solution.py:52
  61.3 34.6 %all-gather.5.cloned.1.call-done = bf16[512,4096]{1,0:T(8,128)(2,1)} async-done(((bf16[128,4096]{1,0:T(8,128)(2,1)}), bf16[512,4096]{1,0:T(8,128)(2,1)}) %all-gather.5.cloned.1.call-update) | async-done | bytes 4194320 | tf_op jit(solution)/shard_map/all_gather | solution.py:46
  95.9 4.2 %fusion.27 = f32[512,256]{0,1:T(8,128)S(1)} fusion(bf16[512,4096]{1,0:T(8,128)(2,1)} %all-gather.5.cloned.1.call-done, bf16[512,8,2,128]{3,2,1,0:T(2,128)(2,1)} %bitcast.161), kind=kOutput, calls=%fused_computation.38 | convolution fusion | flops 1073741824 | bytes 6815744 | tf_op jit(solution)/shard_map/dot_general | solution.py:56
  100.1 0.6 fusion.48
  100.7 0.2 copy-done
  100.9 0.8 copy.35
  101.7 69.1 %all-gather.9.cloned.1.call-done = bf16[4096,512]{1,0:T(8,128)(2,1)} async-done(((bf16[512,512]{1,0:T(8,128)(2,1)}), bf16[4096,512]{1,0:T(8,128)(2,1)}) %all-gather.9.cloned.1.call-update) | async-done | bytes 4194320 | tf_op jit(solution)/shard_map/all_gather | solution.py:51
  170.8 5.8 %fusion.64 = f32[512,512]{0,1:T(8,128)S(1)} fusion(bf16[512,4096]{1,0:T(8,128)(2,1)} %all-gather.5.cloned.1.call-done, bf16[4096,512]{1,0:T(8,128)(2,1)} %all-gather.9.cloned.1.call-done), kind=kOutput, calls=%fused_computation.92 | convolution fusion | flops 2147483648 | bytes 9437184 | tf_op jit(solution)/shard_map/dot_general | solution.py:55
  176.7 0.1 fusion.63
  176.8 0.3 copy.43
  177.1 0.3 copy.44
  177.5 0.3 subtract_convert_fusion
  177.8 0.3 pad_maximum_fusion
  178.1 1.2 fusion.21
  179.3 1.0 fusion.23
  180.4 1.6 fusion.36
  182.0 29.8 %while.22 = (s32[]{:T(128)}, bf16[512,2,1,128]{3,0,2,1:T(8,128)(2,1)S(1)}, f32[1,4,512]{2,1,0:T(4,128)S(1)}, f32[1,4,512]{2,1,0:T(4,128)S(1)}, f32[1,4,512,128]{...) while((s32[]{:T(128)}, ...), condition=%wide.region_10.11_spmd.clone, body=%wide.region_6.10_spmd.clone.sunk | while | flops 552107520 | bytes 18236672 | solution.py:119
  182.2 2.5 collective-permute-start
  184.7 0.1 convert_reduce_fusion.2
  184.8 0.3 compare_and_fusion.3
  185.1 6.1 %collective-permute-done = bf16[512,2,1,128]{3,0,2,1:T(8,128)(2,1)S(1)} collective-permute-done((bf16[512,2,1,128]{3,0,2,1:T(8,128)(2,1)S(1)}, bf16[512,2,1,128]{3,0,2,1:T(8,128)(2,1)S(1)}, u32[]{:S(2)}, u32[]{:S(2)}) %collective-permute-start) | collective-permute-done | bytes 262176 | tf_op jit(solution)/shard_map/while/body/eval_jaxpr/ppermute | solution.py:15
  191.2 0.9 fusion.76
  192.1 1.0 fusion.78
  193.2 1.9 fusion.79
  195.2 8.8 %collective-permute-start = (bf16[512,2,1,128]{3,0,2,1:T(8,128)(2,1)S(1)}, bf16[512,2,1,128]{3,0,2,1:T(8,128)(2,1)S(1)}, u32[]{:S(2)}, u32[]{:S(2)}) collective-permute-start(bf16[512,2,1,128]{3,0,2,1:T(8,128)(2,1)S(1)} %get-tuple-element.431), channel_id=1, source_target_pairs={{0,1},{1,2},{2,3},{3,4},{4,5},{5,6},{6,7},{8,9},{9,10},{10,11},{11... | collective-permute-start | bytes 786440 | tf_op jit(solution)/shard_map/while/body/eval_jaxpr/ppermute | solution.py:15
  204.0 0.1 convert_reduce_fusion.2
  204.1 0.3 compare_and_fusion.3
  204.4 3.4 %collective-permute-done = bf16[512,2,1,128]{3,0,2,1:T(8,128)(2,1)S(1)} collective-permute-done((bf16[512,2,1,128]{3,0,2,1:T(8,128)(2,1)S(1)}, bf16[512,2,1,128]{3,0,2,1:T(8,128)(2,1)S(1)}, u32[]{:S(2)}, u32[]{:S(2)}) %collective-permute-start) | collective-permute-done | bytes 262176 | tf_op jit(solution)/shard_map/while/body/eval_jaxpr/ppermute | solution.py:15
  207.8 0.9 fusion.76
  208.7 1.0 fusion.78
  209.8 1.9 fusion.79
  211.7 0.3 copy.36
  212.1 0.1 divide_convert_fusion
  212.2 41.3 %all-gather.11.cloned.1.call-done = bf16[512,4096]{1,0:T(8,128)(2,1)} async-done(((bf16[64,4096]{1,0:T(8,128)(2,1)}), bf16[512,4096]{1,0:T(8,128)(2,1)}) %all-gather.11.cloned.1.call-update) | async-done | bytes 4194320 | tf_op jit(solution)/shard_map/all_gather | solution.py:123
  253.6 6.5 %convolution_convert_fusion = bf16[512,4096]{1,0:T(8,128)(2,1)} fusion(bf16[512,512]{0,1:T(8,128)(2,1)S(1)} %bitcast.151, bf16[512,4096]{1,0:T(8,128)(2,1)} %all-gather.11.cloned.1.call-done), kind=kOutput, calls=%fused_computation.27 | convolution fusion | flops 2149580800 | bytes 8912896 | tf_op jit(solution)/shard_map/dot_general | solution.py:125
  260.1 45.2 %reduce-scatter.2.cloned.1.call-done = bf16[128,4096]{1,0:T(8,128)(2,1)} async-done(((bf16[512,4096]{1,0:T(8,128)(2,1)}), bf16[128,4096]{1,0:T(8,128)(2,1)}) %reduce-scatter.2.cloned.1.call-update) | async-done | bytes 1048592 | tf_op jit(solution)/shard_map/reduce_scatter | solution.py:124
  (33 shorter events, 0.3 us)
Async XLA Ops:
  6.5 6.2 %copy-start.3 = (s32[16]{0:T(128)S(1)}, s32[16]{0:T(128)}, u32[]{:S(2)}) copy-start(s32[16]{0:T(128)} %param.11) | copy-start | bytes 196
  6.5 54.8 %all-gather.7.cloned.1.call-start = ((), (), s32[]{:S(2)}) async-start(), calls=%async_computation.2 | async-start | bytes 2359296 | tf_op jit(solution)/shard_map/all_gather | solution.py:52
  7.3 88.6 %all-gather.5.cloned.1.call-start = ((), (), s32[]{:S(2)}) async-start(), calls=%async_computation.1 | async-start | bytes 5242880 | tf_op jit(solution)/shard_map/all_gather | solution.py:46
  11.3 159.5 %all-gather.9.cloned.1.call-start = ((), (), s32[]{:S(2)}) async-start(), calls=%async_computation.3 | async-start | bytes 4718592 | tf_op jit(solution)/shard_map/all_gather | solution.py:51
  12.1 241.5 %all-gather.11.cloned.1.call-start = ((), (), s32[]{:S(2)}) async-start(), calls=%async_computation.4 | async-start | bytes 4718592 | tf_op jit(solution)/shard_map/all_gather | solution.py:123
  12.6 292.7 %reduce-scatter.2.cloned.1.call-start = ((), (), s32[]{:S(2)}) async-start(), calls=%async_computation.5 | async-start | bytes 5242880 | tf_op jit(solution)/shard_map/reduce_scatter | solution.py:124
  100.0 0.8 copy-start
  178.1 2.3 copy-start.1
  180.4 1.6 copy-start.2
  182.2 9.1 %collective-permute-start = (bf16[512,2,1,128]{3,0,2,1:T(8,128)(2,1)S(1)}, bf16[512,2,1,128]{3,0,2,1:T(8,128)(2,1)S(1)}, u32[]{:S(2)}, u32[]{:S(2)}) collective-permute-start(bf16[512,2,1,128]{3,0,2,1:T(8,128)(2,1)S(1)} %get-tuple-element.431), channel_id=1, source_target_pairs={{0,1},{1,2},{2,3},{3,4},{4,5},{5,6},{6,7},{8,9},{9,10},{10,11},{11... | collective-permute-start | bytes 786440 | tf_op jit(solution)/shard_map/while/body/eval_jaxpr/ppermute | solution.py:15
  195.2 12.7 %collective-permute-start = (bf16[512,2,1,128]{3,0,2,1:T(8,128)(2,1)S(1)}, bf16[512,2,1,128]{3,0,2,1:T(8,128)(2,1)S(1)}, u32[]{:S(2)}, u32[]{:S(2)}) collective-permute-start(bf16[512,2,1,128]{3,0,2,1:T(8,128)(2,1)S(1)} %get-tuple-element.431), channel_id=1, source_target_pairs={{0,1},{1,2},{2,3},{3,4},{4,5},{5,6},{6,7},{8,9},{9,10},{10,11},{11... | collective-permute-start | bytes 786440 | tf_op jit(solution)/shard_map/while/body/eval_jaxpr/ppermute | solution.py:15
Sparse Core Ops, SparseCore 0:
  9.5 51.7 all-gather.6
  62.9 32.9 all-gather.4
  98.0 72.7 all-gather.8
  172.8 80.7 all-gather.10
  260.2 45.0 reduce-scatter.1
where the time goes:
time: 312 us
  waiting for transfers between devices  249 us (80%)
  matrix products  24.9 us (8%)
  between operations  13.3 us (4%)
  starting transfers between devices  11.4 us (4%)
  other arithmetic  11 us (4%)
    all_gather x1, waiting for transfers between devices, on_device(): lax.all_gather(w_query, 'blk', axis=0, tiled=True)  69.1 us
    all_gather x1, waiting for transfers between devices, on_device(): lax.all_gather(key_value_weight, 'blk', axis=0, tiled=True)  46.9 us
    reduce_scatter x1, waiting for transfers between devices, on_device(): lax.psum_scatter(jnp.dot(mixed, head_rows, preferred_element_type=jnp.flo...  45.2 us
    all_gather x1, waiting for transfers between devices, on_device(): head_rows = lax.all_gather(w_out, 'blk', axis=0, tiled=True)  41.3 us
    all_gather x1, waiting for transfers between devices, on_device(): block_input = lax.all_gather(normalized_input, 'heads', axis=0, tiled=True)  34.6 us
    ppermute x2, starting transfers between devices, shifted(): lax.ppermute(value, axis, [(source, source + steps) for source in range(f...  11.3 us
    ppermute x2, waiting for transfers between devices, shifted(): lax.ppermute(value, axis, [(source, source + steps) for source in range(f...  9.5 us
    dot_general x1, matrix products, on_device(): jnp.dot(mixed, head_rows, preferred_element_type=jnp.float32)  6.52 us
  transfers between devices with their start and end apart: 7, of which 7 were waited for; matrix products, arithmetic and copies ran while one was open for 10% of the time, Pallas kernels for 0%

commit v1 on v0

--- a/solution.py
+++ b/solution.py
@@ -47,9 +47,16 @@
     block_rows = block_input.shape[0]
     query_cols = w_query.shape[1]
     kv_cols = key_value_weight.shape[2]
+
+    def extend_weights_here(array_in):
+        carry_in = jnp.concatenate(
+            lax.all_to_all(jnp.stack(lax.axis_size("blk") * [array_in]), "blk", 0, 0), 0
+        )
+        return carry_in
+
     pieces = (
         lax.all_gather(w_query, "blk", axis=0, tiled=True),
-        lax.all_gather(key_value_weight, "blk", axis=0, tiled=True),
+        extend_weights_here(key_value_weight),
     )
     count = pieces[0].shape[0]
     query_part = jnp.dot(block_input, pieces[0], preferred_element_type=jnp.float32)

time: 312 us -> 271 us (0.87)
  waiting for transfers between devices: 249 us -> 199 us
  starting transfers between devices: 11.4 us -> 18.5 us
    all_to_all x0 -> x1, waiting for transfers between devices: none -> 62.6 us  [extend_weights_here(): lax.all_to_all(jnp.stack(lax.axis_size('blk') * [array_in]), 'blk', 0, 0)]
    all_gather x1 -> x0, waiting for transfers between devices: 46.9 us -> none  [on_device(): lax.all_gather(key_value_weight, 'blk', axis=0, tiled=True)]
    all_gather x1, waiting for transfers between devices: 34.6 us -> 0.01 us  [on_device(): block_input = lax.all_gather(normalized_input, 'heads', axis=0, tiled=True)]
    all_gather x1, waiting for transfers between devices: 69.1 us -> 38.8 us  [on_device(): lax.all_gather(w_query, 'blk', axis=0, tiled=True)]
    all_to_all x0 -> x1, starting transfers between devices: none -> 7.28 us  [extend_weights_here(): lax.all_to_all(jnp.stack(lax.axis_size('blk') * [array_in]), 'blk', 0, 0)]
  transfers between devices with their start and end apart: 7 -> 7, of which waited for: 7 -> 6; matrix products, arithmetic and copies ran while one was open for 10% -> 11% of each run, Pallas kernels for 0% -> 0%
where the time goes in v1:
time: 271 us
  waiting for transfers between devices  199 us (73%)
  matrix products  24.2 us (9%)
  starting transfers between devices  18.5 us (7%)
  between operations  13.3 us (5%)
  other arithmetic  11.1 us (4%)
  local copies, waits for them, and re-layouts  4.64 us (2%)
    all_to_all x1, waiting for transfers between devices, extend_weights_here(): lax.all_to_all(jnp.stack(lax.axis_size('blk') * [array_in]), 'blk', 0, 0)  62.6 us
    reduce_scatter x1, waiting for transfers between devices, on_device(): lax.psum_scatter(jnp.dot(mixed, head_rows, preferred_element_type=jnp.flo...  45.1 us
    all_gather x1, waiting for transfers between devices, on_device(): head_rows = lax.all_gather(w_out, 'blk', axis=0, tiled=True)  41.4 us
    all_gather x1, waiting for transfers between devices, on_device(): lax.all_gather(w_query, 'blk', axis=0, tiled=True)  38.8 us
    ppermute x2, starting transfers between devices, shifted(): lax.ppermute(value, axis, [(source, source + steps) for source in range(f...  11.1 us
    ppermute x2, waiting for transfers between devices, shifted(): lax.ppermute(value, axis, [(source, source + steps) for source in range(f...  9.66 us
    all_to_all x1, starting transfers between devices, extend_weights_here(): lax.all_to_all(jnp.stack(lax.axis_size('blk') * [array_in]), 'blk', 0, 0)  7.28 us
    dot_general x1, matrix products, on_device(): jnp.dot(mixed, head_rows, preferred_element_type=jnp.float32)  6.52 us
  transfers between devices with their start and end apart: 7, of which 6 were waited for; matrix products, arithmetic and copies ran while one was open for 11% of the time, Pallas kernels for 0%

profile of v1, /device:TPU:0, one launch (start us, length us, event | category | flops | bytes accessed | tf_op | source)
XLA Modules:
  0.0 271.1 jit_solution(4300637683087617391)
XLA Ops:
  6.5 1.6 fusion.24
  8.1 2.5 fusion.25
  10.6 0.0 all-gather.6.cloned.1.call-start
  10.6 0.7 all-gather.6.cloned.1.call-update
  11.4 2.4 stack.6
  13.8 7.3 %all-to-all-start = ((bf16[8,512,2,128]{3,2,1,0:T(2,128)(2,1)}), bf16[8,512,2,128]{3,2,1,0:T(2,128)(2,1)S(1)}, u32[]{:S(2)}, u32[]{:S(2)}) async-start(bf16[8,512,2,128]{3,2,1,0:T(2,128)(2,1)} %stack.6), calls=%async_computation | async-start | bytes 4194304 | tf_op jit(solution)/shard_map/all_to_all | solution.py:53
  21.1 0.0 all-gather.8.cloned.1.call-start
  21.1 0.7 all-gather.8.cloned.1.call-update
  21.8 0.0 reduce-scatter.2.cloned.1.call-start
  21.9 0.2 broadcast_in_dim.114
  22.1 0.1 fusion.56
  22.2 0.3 compare_and_fusion.1
  22.5 1.0 multiply_cosine_fusion
  23.5 62.6 %all-to-all-done = bf16[8,512,2,128]{3,2,1,0:T(2,128)(2,1)S(1)} async-done(((bf16[8,512,2,128]{3,2,1,0:T(2,128)(2,1)}), bf16[8,512,2,128]{3,2,1,0:T(2,128)(2,1)S(1)}, u32[]{:S(2)}, u32[]{:S(2)}) %all-to-all-start) | async-done | bytes 2097184 | tf_op jit(solution)/shard_map/all_to_all | solution.py:53
  86.2 3.5 %fusion.27 = f32[512,256]{0,1:T(8,128)S(1)} fusion(bf16[512,4096]{1,0:T(8,128)(2,1)} %all-gather.4.cloned.1.call-done, bf16[512,8,2,128]{3,2,1,0:T(2,128)(2,1)S(1)} %bitcast.153), kind=kOutput, calls=%fused_computation.38 | convolution fusion | flops 1073741824 | bytes 6815744 | tf_op jit(solution)/shard_map/dot_general | solution.py:63
  89.7 0.6 fusion.48
  90.3 0.2 copy-done
  90.5 0.8 copy.27
  91.3 38.8 %all-gather.6.cloned.1.call-done = bf16[4096,512]{1,0:T(8,128)(2,1)} async-done(((bf16[512,512]{1,0:T(8,128)(2,1)}), bf16[4096,512]{1,0:T(8,128)(2,1)}) %all-gather.6.cloned.1.call-update) | async-done | bytes 4194320 | tf_op jit(solution)/shard_map/all_gather | solution.py:58
  130.1 5.8 %fusion.64 = f32[512,512]{0,1:T(8,128)S(1)} fusion(bf16[512,4096]{1,0:T(8,128)(2,1)} %all-gather.4.cloned.1.call-done, bf16[4096,512]{1,0:T(8,128)(2,1)} %all-gather.6.cloned.1.call-done), kind=kOutput, calls=%fused_computation.92 | convolution fusion | flops 2147483648 | bytes 9437184 | tf_op jit(solution)/shard_map/dot_general | solution.py:62
  136.0 0.1 fusion.63
  136.1 0.3 copy.35
  136.4 0.3 copy.36
  136.8 0.3 subtract_convert_fusion
  137.1 0.3 pad_maximum_fusion
  137.4 1.2 fusion.21
  138.6 1.0 fusion.23
  139.7 1.6 fusion.36
  141.3 29.8 %while.22 = (s32[]{:T(128)}, bf16[512,2,1,128]{3,0,2,1:T(8,128)(2,1)S(1)}, f32[1,4,512]{2,1,0:T(4,128)S(1)}, f32[1,4,512]{2,1,0:T(4,128)S(1)}, f32[1,4,512,128]{...) while((s32[]{:T(128)}, ...), condition=%wide.region_10.11_spmd.clone, body=%wide.region_6.10_spmd.clone.sunk | while | flops 552107520 | bytes 18236672 | solution.py:126
  141.5 2.5 collective-permute-start
  144.0 0.1 convert_reduce_fusion.2
  144.1 0.3 compare_and_fusion.3
  144.4 6.3 %collective-permute-done = bf16[512,2,1,128]{3,0,2,1:T(8,128)(2,1)S(1)} collective-permute-done((bf16[512,2,1,128]{3,0,2,1:T(8,128)(2,1)S(1)}, bf16[512,2,1,128]{3,0,2,1:T(8,128)(2,1)S(1)}, u32[]{:S(2)}, u32[]{:S(2)}) %collective-permute-start) | collective-permute-done | bytes 262176 | tf_op jit(solution)/shard_map/while/body/eval_jaxpr/ppermute | solution.py:15
  150.7 0.9 fusion.76
  151.6 1.0 fusion.78
  152.7 1.9 fusion.79
  154.6 8.6 %collective-permute-start = (bf16[512,2,1,128]{3,0,2,1:T(8,128)(2,1)S(1)}, bf16[512,2,1,128]{3,0,2,1:T(8,128)(2,1)S(1)}, u32[]{:S(2)}, u32[]{:S(2)}) collective-permute-start(bf16[512,2,1,128]{3,0,2,1:T(8,128)(2,1)S(1)} %get-tuple-element.421), channel_id=1, source_target_pairs={{0,1},{1,2},{2,3},{3,4},{4,5},{5,6},{6,7},{8,9},{9,10},{10,11},{11... | collective-permute-start | bytes 786440 | tf_op jit(solution)/shard_map/while/body/eval_jaxpr/ppermute | solution.py:15
  163.3 0.1 convert_reduce_fusion.2
  163.4 0.3 compare_and_fusion.3
  163.7 3.4 %collective-permute-done = bf16[512,2,1,128]{3,0,2,1:T(8,128)(2,1)S(1)} collective-permute-done((bf16[512,2,1,128]{3,0,2,1:T(8,128)(2,1)S(1)}, bf16[512,2,1,128]{3,0,2,1:T(8,128)(2,1)S(1)}, u32[]{:S(2)}, u32[]{:S(2)}) %collective-permute-start) | collective-permute-done | bytes 262176 | tf_op jit(solution)/shard_map/while/body/eval_jaxpr/ppermute | solution.py:15
  167.1 0.9 fusion.76
  168.0 1.0 fusion.78
  169.1 1.9 fusion.79
  171.0 0.3 copy.28
  171.4 0.1 divide_convert_fusion
  171.5 41.4 %all-gather.8.cloned.1.call-done = bf16[512,4096]{1,0:T(8,128)(2,1)} async-done(((bf16[64,4096]{1,0:T(8,128)(2,1)}), bf16[512,4096]{1,0:T(8,128)(2,1)}) %all-gather.8.cloned.1.call-update) | async-done | bytes 4194320 | tf_op jit(solution)/shard_map/all_gather | solution.py:130
  212.9 6.5 %convolution_convert_fusion = bf16[512,4096]{1,0:T(8,128)(2,1)} fusion(bf16[512,512]{0,1:T(8,128)(2,1)S(1)} %bitcast.152, bf16[512,4096]{1,0:T(8,128)(2,1)} %all-gather.8.cloned.1.call-done), kind=kOutput, calls=%fused_computation.27 | convolution fusion | flops 2149580800 | bytes 8912896 | tf_op jit(solution)/shard_map/dot_general | solution.py:132
  219.5 45.1 %reduce-scatter.2.cloned.1.call-done = bf16[128,4096]{1,0:T(8,128)(2,1)} async-done(((bf16[512,4096]{1,0:T(8,128)(2,1)}), bf16[128,4096]{1,0:T(8,128)(2,1)}) %reduce-scatter.2.cloned.1.call-update) | async-done | bytes 1048592 | tf_op jit(solution)/shard_map/reduce_scatter | solution.py:131
  (35 shorter events, 0.3 us)
Async XLA Ops:
  6.5 4.8 %copy-start.2 = (bf16[512,2,128]{2,1,0:T(2,128)(2,1)S(1)}, bf16[512,2,128]{2,1,0:T(2,128)(2,1)}, u32[]{:S(2)}) copy-start(bf16[512,2,128]{2,1,0:T(2,128)(2,1)} %param.9) | copy-start | bytes 786436
  6.5 79.6 %all-gather.4.cloned.1.call-start = ((), (), s32[]{:S(2)}) async-start(), calls=%async_computation.2 | async-start | bytes 5242880 | tf_op jit(solution)/shard_map/all_gather | solution.py:46
  10.6 11.3 %copy-start.4 = (s32[16]{0:T(128)S(1)}, s32[16]{0:T(128)}, u32[]{:S(2)}) copy-start(s32[16]{0:T(128)} %param.11) | copy-start | bytes 196
  10.6 119.5 %all-gather.6.cloned.1.call-start = ((), (), s32[]{:S(2)}) async-start(), calls=%async_computation.3 | async-start | bytes 4718592 | tf_op jit(solution)/shard_map/all_gather | solution.py:58
  13.8 72.4 %all-to-all-start = ((bf16[8,512,2,128]{3,2,1,0:T(2,128)(2,1)}), bf16[8,512,2,128]{3,2,1,0:T(2,128)(2,1)S(1)}, u32[]{:S(2)}, u32[]{:S(2)}) async-start(bf16[8,512,2,128]{3,2,1,0:T(2,128)(2,1)} %stack.6), calls=%async_computation | async-start | bytes 4194304 | tf_op jit(solution)/shard_map/all_to_all | solution.py:53
  21.1 191.9 %all-gather.8.cloned.1.call-start = ((), (), s32[]{:S(2)}) async-start(), calls=%async_computation.4 | async-start | bytes 4718592 | tf_op jit(solution)/shard_map/all_gather | solution.py:130
  21.8 242.8 %reduce-scatter.2.cloned.1.call-start = ((), (), s32[]{:S(2)}) async-start(), calls=%async_computation.5 | async-start | bytes 5242880 | tf_op jit(solution)/shard_map/reduce_scatter | solution.py:131
  89.6 0.8 copy-start
  137.4 2.3 copy-start.1
  139.7 1.6 copy-start.3
  141.5 9.2 %collective-permute-start = (bf16[512,2,1,128]{3,0,2,1:T(8,128)(2,1)S(1)}, bf16[512,2,1,128]{3,0,2,1:T(8,128)(2,1)S(1)}, u32[]{:S(2)}, u32[]{:S(2)}) collective-permute-start(bf16[512,2,1,128]{3,0,2,1:T(8,128)(2,1)S(1)} %get-tuple-element.421), channel_id=1, source_target_pairs={{0,1},{1,2},{2,3},{3,4},{4,5},{5,6},{6,7},{8,9},{9,10},{10,11},{11... | collective-permute-start | bytes 786440 | tf_op jit(solution)/shard_map/while/body/eval_jaxpr/ppermute | solution.py:15
  154.6 12.5 %collective-permute-start = (bf16[512,2,1,128]{3,0,2,1:T(8,128)(2,1)S(1)}, bf16[512,2,1,128]{3,0,2,1:T(8,128)(2,1)S(1)}, u32[]{:S(2)}, u32[]{:S(2)}) collective-permute-start(bf16[512,2,1,128]{3,0,2,1:T(8,128)(2,1)S(1)} %get-tuple-element.421), channel_id=1, source_target_pairs={{0,1},{1,2},{2,3},{3,4},{4,5},{5,6},{6,7},{8,9},{9,10},{10,11},{11... | collective-permute-start | bytes 786440 | tf_op jit(solution)/shard_map/while/body/eval_jaxpr/ppermute | solution.py:15
Sparse Core Ops, SparseCore 0:
  10.7 37.1 all-gather.3
  50.1 80.0 all-gather.5
  132.3 80.6 all-gather.7
  219.6 44.9 reduce-scatter.1
